TPU v7x, 32 devices: a whole 2x2x4 slice. The times are simulated.
32 devices in a mesh: gz: 32 (over z, y, x, core).
Axes of the slice: x: 2, y: 2, z: 4, core: 2. Of those that a mesh axis runs over, the one named last changes fastest.
Arguments:
- state: float32 [8, 32, 64, 256], P(None, 'gz'), may hold values from -18 to 18
- explicit_rhs: float32 [2, 8, 32, 64, 256], P(None, None, 'gz'), may hold values from -6 to 6
- implicit_rhs: float32 [2, 8, 32, 64, 256], P(None, None, 'gz'), may hold values from -6 to 6
- implicit_coef: float32 [8], replicated, may hold values from 0.5 to 4
Outputs:
- section_value: float32 [8, 32, 64, 256], P(None, 'gz')
- weighted_rms: float32 [], replicated
All inputs are finite; a program needn't handle non-finite values.
Results may differ from a plain program's by a relative error of at most 0.0001.
Values sent between devices are 32-bit elements; how exact they have to be, the bound alone decides.
No kernel may reach another device: no remote copies, remote signals or barrier semaphores. Data moves between devices by JAX's collectives and lax.ppermute only.
A program may use at most 64 MiB of HBM per device.

v0:
```python
import jax
import jax.numpy as jnp
from jax import lax
from jax.sharding import PartitionSpec as P

ITERS = 3


explicit_weights = (5535828885825.0 / 10492691773637.0, 788022342437.0 / 10882634858940.0)
implicit_weights = (2746238789719.0 / 10658868560708.0, -640167445237.0 / 6845629431997.0)


def extended(block, sides, width):
    for axis, dim in sides:
        count = lax.axis_size(axis)
        forward = [(i, i + 1) for i in range(count - 1)]
        forward.append((count - 1, 0))
        backward = [(target, source) for source, target in forward]
        low = lax.ppermute(
            lax.slice_in_dim(block, block.shape[dim] - width, None, axis=dim), axis, forward
        )
        high = lax.ppermute(lax.slice_in_dim(block, 0, width, axis=dim), axis, backward)
        block = jnp.concatenate([low, block, high], axis=dim)
    return block


def operate(field, implicit_coef):
    padded = extended(field, (("gz", 1),), 1)
    flat = jnp.pad(field, ((0, 0), (0, 0), (1, 1), (1, 1)))
    beside = padded[:, 2:] + padded[:, :-2]
    beside = (
        beside
        + flat[:, :, 2:, 1:-1]
        + flat[:, :, :-2, 1:-1]
        + flat[:, :, 1:-1, 2:]
        + flat[:, :, 1:-1, :-2]
    )
    return field - implicit_coef[:, None, None, None] * (beside - 6.0 * field)


def species_sum(first, second):
    return jnp.sum(first * second, axis=(1, 2, 3))


def widen(values):
    return values[:, None, None, None]


def paired_totals(residual, image):
    return lax.psum((species_sum(residual, residual), species_sum(residual, image)), "gz")


def shards(state, explicit_rhs, implicit_rhs, implicit_coef):
    section_in = (
        state + explicit_weights[0] * explicit_rhs[0] + explicit_weights[1] * explicit_rhs[1]
    )
    section_in = (
        section_in + implicit_weights[0] * implicit_rhs[0] + implicit_weights[1] * implicit_rhs[1]
    )
    solution = section_in
    residual = section_in - operate(section_in, implicit_coef)
    image = operate(residual, implicit_coef)
    norm_now, product = paired_totals(residual, image)
    step_size = norm_now / product
    direction, along = (residual, image)
    for iteration in range(ITERS):
        solution = solution + widen(step_size) * direction
        residual = residual - widen(step_size) * along
        if iteration + 1 < ITERS:
            image = operate(residual, implicit_coef)
            norm_next, product = paired_totals(residual, image)
            beta_ratio = norm_next / norm_now
            step_size = norm_next / (product - beta_ratio * norm_next / step_size)
            direction = residual + widen(beta_ratio) * direction
            along = image + widen(beta_ratio) * along
            norm_now = norm_next
    scaled = (solution - section_in) / (1.0 + 0.1 * jnp.abs(state))
    summed = lax.psum(jnp.sum(scaled * scaled), "gz")
    cells = state.shape[0] * state.shape[1] * state.shape[2] * state.shape[3] * lax.axis_size("gz")
    weighted_rms = jnp.sqrt(summed / cells)
    return (solution, weighted_rms)


def solution(mesh):
    placed = (
        P(None, "gz", None, None),
        P(None, None, "gz", None, None),
        P(None, None, "gz", None, None),
        P(),
    )
    return jax.shard_map(
        shards,
        mesh=mesh,
        in_specs=placed,
        out_specs=(P(None, "gz", None, None), P()),
        check_vma=False,
    )
```

profile of v0, /device:TPU:0, one launch (start us, length us, event | category | flops | bytes accessed | tf_op | source)
XLA Modules:
  0.0 231.7 jit_solution(5096243055173741715)
XLA Ops:
  0.6 0.0 copy-start.1
  0.6 1.9 fusion.28
  2.5 0.5 collective-permute-start.1
  3.1 6.0 %collective-permute-start = (f32[8,1,64,256]{3,2,1,0:T(8,128)S(1)}, f32[8,1,64,256]{3,2,1,0:T(8,128)S(1)}, u32[]{:S(2)}, u32[]{:S(2)}) collective-permute-start(f32[8,1,64,256]{3,2,1,0:T(8,128)S(1)} %fusion.28), channel_id=1, source_target_pairs={{1,0},{2,1},{3,2},{4,3},{5,4},{6,5},{7,6},{8,7},{9,8},{10,9},{11,1... | collective-permute-start | bytes 1572872 | tf_op jit(solution)/shard_map/ppermute | solution.py:22
  9.0 6.9 %collective-permute-done.1 = f32[8,1,64,256]{3,2,1,0:T(8,128)S(1)} collective-permute-done((f32[8,1,64,256]{3,2,1,0:T(8,128)S(1)}, f32[8,1,64,256]{3,2,1,0:T(8,128)S(1)}, u32[]{:S(2)}, u32[]{:S(2)}) %collective-permute-start.1) | collective-permute-done | bytes 524320 | tf_op jit(solution)/shard_map/ppermute | solution.py:19
  15.9 0.0 collective-permute-done
  15.9 0.0 copy-done.1
  15.9 0.4 subtract_subtract_fusion
  16.4 3.2 %collective-permute-start.3 = (f32[8,1,64,256]{3,2,1,0:T(8,128)S(1)}, f32[8,1,64,256]{3,2,1,0:T(8,128)S(1)}, u32[]{:S(2)}, u32[]{:S(2)}) collective-permute-start(f32[8,1,64,256]{3,2,1,0:T(8,128)S(1)} %subtract_subtract_fusion), channel_id=1, source_target_pairs={{0,1},{1,2},{2,3},{3,4},{4,5},{5,6},{6,7},{7,8},{8,9},{9,10},{10,1... | collective-permute-start | bytes 1572872 | tf_op jit(solution)/shard_map/ppermute | solution.py:19
  19.5 2.4 %collective-permute-start.2 = (f32[8,1,64,256]{3,2,1,0:T(8,128)S(1)}, f32[8,1,64,256]{3,2,1,0:T(8,128)S(1)}, u32[]{:S(2)}, u32[]{:S(2)}) collective-permute-start(f32[8,1,64,256]{3,2,1,0:T(8,128)S(1)} %subtract_subtract_fusion), channel_id=1, source_target_pairs={{1,0},{2,1},{3,2},{4,3},{5,4},{6,5},{7,6},{8,7},{9,8},{10,9},{11,1... | collective-permute-start | bytes 1572872 | tf_op jit(solution)/shard_map/ppermute | solution.py:22
  21.9 6.9 %collective-permute-done.3 = f32[8,1,64,256]{3,2,1,0:T(8,128)S(1)} collective-permute-done((f32[8,1,64,256]{3,2,1,0:T(8,128)S(1)}, f32[8,1,64,256]{3,2,1,0:T(8,128)S(1)}, u32[]{:S(2)}, u32[]{:S(2)}) %collective-permute-start.3) | collective-permute-done | bytes 524320 | tf_op jit(solution)/shard_map/ppermute | solution.py:19
  28.8 0.0 collective-permute-done.2
  28.8 0.5 multiply_reduce_fusion.4
  29.3 48.9 %all-reduce.6 = (f32[8]{0:T(128)S(1)}, f32[8]{0:T(128)S(1)}) all-reduce(f32[8]{0:T(128)S(1)} %get-tuple-element.7, f32[8]{0:T(128)S(1)} %get-tuple-element.6), channel_id=1, replica_groups=mesh['gz'=32] {'gz'}, use_global_device_ids=true, to_apply=%region_1.2 | all-reduce | flops 16 | bytes 128 | tf_op jit(solution)/shard_map/psum | solution.py:50
  78.2 0.1 multiply_subtract_fusion.1
  78.4 0.1 collective-permute-start.5
  78.4 5.3 %collective-permute-start.4 = (f32[8,1,64,256]{3,2,1,0:T(8,128)S(1)}, f32[8,1,64,256]{3,2,1,0:T(8,128)S(1)}, u32[]{:S(2)}, u32[]{:S(2)}) collective-permute-start(f32[8,1,64,256]{3,2,1,0:T(8,128)S(1)} %multiply_subtract_fusion.1), channel_id=1, source_target_pairs={{1,0},{2,1},{3,2},{4,3},{5,4},{6,5},{7,6},{8,7},{9,8},{10,9},{11,1... | collective-permute-start | bytes 1572872 | tf_op jit(solution)/shard_map/ppermute | solution.py:22
  83.8 7.0 %collective-permute-done.5 = f32[8,1,64,256]{3,2,1,0:T(8,128)S(1)} collective-permute-done((f32[8,1,64,256]{3,2,1,0:T(8,128)S(1)}, f32[8,1,64,256]{3,2,1,0:T(8,128)S(1)}, u32[]{:S(2)}, u32[]{:S(2)}) %collective-permute-start.5) | collective-permute-done | bytes 524320 | tf_op jit(solution)/shard_map/ppermute | solution.py:19
  90.7 0.0 collective-permute-done.4
  90.7 0.6 multiply_reduce_fusion.2
  91.3 41.7 %all-reduce.5 = (f32[8]{0:T(128)S(1)}, f32[8]{0:T(128)S(1)}) all-reduce(f32[8]{0:T(128)S(1)} %get-tuple-element.5, f32[8]{0:T(128)S(1)} %get-tuple-element.4), channel_id=1, replica_groups=mesh['gz'=32] {'gz'}, use_global_device_ids=true, to_apply=%region_5.6 | all-reduce | flops 16 | bytes 128 | tf_op jit(solution)/shard_map/psum | solution.py:50
  133.0 0.2 multiply_subtract_fusion
  133.2 0.0 copy-start
  133.2 0.1 collective-permute-start.7
  133.2 5.3 %collective-permute-start.6 = (f32[8,1,64,256]{3,2,1,0:T(8,128)S(1)}, f32[8,1,64,256]{3,2,1,0:T(8,128)S(1)}, u32[]{:S(2)}, u32[]{:S(2)}) collective-permute-start(f32[8,1,64,256]{3,2,1,0:T(8,128)S(1)} %multiply_subtract_fusion), channel_id=1, source_target_pairs={{1,0},{2,1},{3,2},{4,3},{5,4},{6,5},{7,6},{8,7},{9,8},{10,9},{11,1... | collective-permute-start | bytes 1572872 | tf_op jit(solution)/shard_map/ppermute | solution.py:22
  138.6 7.0 %collective-permute-done.7 = f32[8,1,64,256]{3,2,1,0:T(8,128)S(1)} collective-permute-done((f32[8,1,64,256]{3,2,1,0:T(8,128)S(1)}, f32[8,1,64,256]{3,2,1,0:T(8,128)S(1)}, u32[]{:S(2)}, u32[]{:S(2)}) %collective-permute-start.7) | collective-permute-done | bytes 524320 | tf_op jit(solution)/shard_map/ppermute | solution.py:19
  145.5 0.0 collective-permute-done.6
  145.5 0.6 fusion
  146.1 41.3 %all-reduce.4 = (f32[8]{0:T(128)S(1)}, f32[8]{0:T(128)S(1)}) all-reduce(f32[8]{0:T(128)S(1)} %get-tuple-element.3, f32[8]{0:T(128)S(1)} %get-tuple-element.2), channel_id=1, replica_groups=mesh['gz'=32] {'gz'}, use_global_device_ids=true, to_apply=%region_9.10 | all-reduce | flops 16 | bytes 128 | tf_op jit(solution)/shard_map/psum | solution.py:50
  187.4 0.0 copy-done
  187.5 1.7 multiply_reduce_fusion
  189.2 40.7 %psum.55 = f32[]{:T(128)} all-reduce(f32[]{:T(128)} %get-tuple-element.14), channel_id=1, replica_groups=mesh['gz'=32] {'gz'}, use_global_device_ids=true, to_apply=%region_13.14 | all-reduce | flops 1 | bytes 8 | tf_op jit(solution)/shard_map/psum | solution.py:78
  (3 shorter events, 0.0 us)
Async XLA Ops:
  0.6 15.3 %copy-start.1 = (f32[8]{0:T(128)S(1)}, f32[8]{0:T(128)}, u32[]{:S(2)}) copy-start(f32[8]{0:T(128)} %param.7) | copy-start | bytes 100
  2.5 13.4 %collective-permute-start.1 = (f32[8,1,64,256]{3,2,1,0:T(8,128)S(1)}, f32[8,1,64,256]{3,2,1,0:T(8,128)S(1)}, u32[]{:S(2)}, u32[]{:S(2)}) collective-permute-start(f32[8,1,64,256]{3,2,1,0:T(8,128)S(1)} %fusion.28), channel_id=1, source_target_pairs={{0,1},{1,2},{2,3},{3,4},{4,5},{5,6},{6,7},{7,8},{8,9},{9,10},{10,1... | collective-permute-start | bytes 1572872 | tf_op jit(solution)/shard_map/ppermute | solution.py:19
  3.1 12.9 %collective-permute-start = (f32[8,1,64,256]{3,2,1,0:T(8,128)S(1)}, f32[8,1,64,256]{3,2,1,0:T(8,128)S(1)}, u32[]{:S(2)}, u32[]{:S(2)}) collective-permute-start(f32[8,1,64,256]{3,2,1,0:T(8,128)S(1)} %fusion.28), channel_id=1, source_target_pairs={{1,0},{2,1},{3,2},{4,3},{5,4},{6,5},{7,6},{8,7},{9,8},{10,9},{11,1... | collective-permute-start | bytes 1572872 | tf_op jit(solution)/shard_map/ppermute | solution.py:22
  16.4 12.4 %collective-permute-start.3 = (f32[8,1,64,256]{3,2,1,0:T(8,128)S(1)}, f32[8,1,64,256]{3,2,1,0:T(8,128)S(1)}, u32[]{:S(2)}, u32[]{:S(2)}) collective-permute-start(f32[8,1,64,256]{3,2,1,0:T(8,128)S(1)} %subtract_subtract_fusion), channel_id=1, source_target_pairs={{0,1},{1,2},{2,3},{3,4},{4,5},{5,6},{6,7},{7,8},{8,9},{9,10},{10,1... | collective-permute-start | bytes 1572872 | tf_op jit(solution)/shard_map/ppermute | solution.py:19
  19.5 9.3 %collective-permute-start.2 = (f32[8,1,64,256]{3,2,1,0:T(8,128)S(1)}, f32[8,1,64,256]{3,2,1,0:T(8,128)S(1)}, u32[]{:S(2)}, u32[]{:S(2)}) collective-permute-start(f32[8,1,64,256]{3,2,1,0:T(8,128)S(1)} %subtract_subtract_fusion), channel_id=1, source_target_pairs={{1,0},{2,1},{3,2},{4,3},{5,4},{6,5},{7,6},{8,7},{9,8},{10,9},{11,1... | collective-permute-start | bytes 1572872 | tf_op jit(solution)/shard_map/ppermute | solution.py:22
  78.4 12.4 %collective-permute-start.5 = (f32[8,1,64,256]{3,2,1,0:T(8,128)S(1)}, f32[8,1,64,256]{3,2,1,0:T(8,128)S(1)}, u32[]{:S(2)}, u32[]{:S(2)}) collective-permute-start(f32[8,1,64,256]{3,2,1,0:T(8,128)S(1)} %multiply_subtract_fusion.1), channel_id=1, source_target_pairs={{0,1},{1,2},{2,3},{3,4},{4,5},{5,6},{6,7},{7,8},{8,9},{9,10},{10,1... | collective-permute-start | bytes 1572872 | tf_op jit(solution)/shard_map/ppermute | solution.py:19
  78.4 12.3 %collective-permute-start.4 = (f32[8,1,64,256]{3,2,1,0:T(8,128)S(1)}, f32[8,1,64,256]{3,2,1,0:T(8,128)S(1)}, u32[]{:S(2)}, u32[]{:S(2)}) collective-permute-start(f32[8,1,64,256]{3,2,1,0:T(8,128)S(1)} %multiply_subtract_fusion.1), channel_id=1, source_target_pairs={{1,0},{2,1},{3,2},{4,3},{5,4},{6,5},{7,6},{8,7},{9,8},{10,9},{11,1... | collective-permute-start | bytes 1572872 | tf_op jit(solution)/shard_map/ppermute | solution.py:22
  133.2 54.3 %copy-start = (f32[8,1,64,256]{3,2,1,0:T(8,128)S(1)}, f32[8,1,64,256]{3,2,1,0:T(8,128)}, u32[]{:S(2)}) copy-start(f32[8,1,64,256]{3,2,1,0:T(8,128)} %param.4) | copy-start | bytes 1572868
  133.2 12.4 %collective-permute-start.7 = (f32[8,1,64,256]{3,2,1,0:T(8,128)S(1)}, f32[8,1,64,256]{3,2,1,0:T(8,128)S(1)}, u32[]{:S(2)}, u32[]{:S(2)}) collective-permute-start(f32[8,1,64,256]{3,2,1,0:T(8,128)S(1)} %multiply_subtract_fusion), channel_id=1, source_target_pairs={{0,1},{1,2},{2,3},{3,4},{4,5},{5,6},{6,7},{7,8},{8,9},{9,10},{10,1... | collective-permute-start | bytes 1572872 | tf_op jit(solution)/shard_map/ppermute | solution.py:19
  133.2 12.3 %collective-permute-start.6 = (f32[8,1,64,256]{3,2,1,0:T(8,128)S(1)}, f32[8,1,64,256]{3,2,1,0:T(8,128)S(1)}, u32[]{:S(2)}, u32[]{:S(2)}) collective-permute-start(f32[8,1,64,256]{3,2,1,0:T(8,128)S(1)} %multiply_subtract_fusion), channel_id=1, source_target_pairs={{1,0},{2,1},{3,2},{4,3},{5,4},{6,5},{7,6},{8,7},{9,8},{10,9},{11,1... | collective-permute-start | bytes 1572872 | tf_op jit(solution)/shard_map/ppermute | solution.py:22
where the time goes:
time: 232 us
  blocking collectives  173 us (75%)
  waiting for transfers between devices  27.7 us (12%)
  starting transfers between devices  22.8 us (10%)
  other arithmetic  5.98 us (3%)
  between operations  2.53 us (1%)
    psum x3, blocking collectives, paired_totals(): lax.psum((species_sum(residual, residual), species_sum(residual, image)),...  132 us
    psum x1, blocking collectives, shards(): summed = lax.psum(jnp.sum(scaled * scaled), 'gz')  40.7 us
    ppermute x4, waiting for transfers between devices, extended(): lax.ppermute(lax.slice_in_dim(block, block.shape[dim] - width, None, axis...  27.7 us
    ppermute x4, starting transfers between devices, extended(): lax.ppermute(lax.slice_in_dim(block, 0, width, axis=dim), axis, backward)  19 us
  transfers between devices with their start and end apart: 8, of which 4 were waited for; matrix products, arithmetic and copies ran while one was open for 0% of the time, Pallas kernels for 0%

commit v1 on v0

v1 whole, which is shorter than its diff:
```python
import jax
import jax.numpy as jnp
from jax import lax
from jax.experimental import pallas as pl
from jax.experimental.pallas import tpu as pltpu
from jax.sharding import PartitionSpec as P

explicit_weights = (5535828885825.0 / 10492691773637.0, 788022342437.0 / 10882634858940.0)
implicit_weights = (2746238789719.0 / 10658868560708.0, -640167445237.0 / 6845629431997.0)

STRIDE = 8


def beside_plane(field):
    rows, cols = field.shape
    row = lax.broadcasted_iota(jnp.int32, field.shape, 0)
    col = lax.broadcasted_iota(jnp.int32, field.shape, 1)
    left = jnp.where(col == 0, 0.0, pltpu.roll(field, 1, 1))
    right = jnp.where(col == cols - 1, 0.0, pltpu.roll(field, cols - 1, 1))
    up = jnp.where(row == 0, 0.0, pltpu.roll(field, 1, 0))
    down = jnp.where(row == rows - 1, 0.0, pltpu.roll(field, rows - 1, 0))
    return (left + right) + (up + down)


def folded(values):
    rows, cols = values.shape
    total = None
    for r in range(0, rows, 8):
        for c in range(0, cols, 128):
            piece = values[r : r + 8, c : c + 128]
            total = piece if total is None else total + piece
    return total


def moments_kernel(own, low, high, low2, high2, far, state, basis, sums, g0, g1, g2, rows):
    half = own.shape[1]
    rows[...] = jnp.zeros(rows.shape, jnp.float32)
    sixth = 1.0 / 6.0

    def species(s, carry):
        def plane(z):
            if z == -3:
                return low2[0, s]
            if z < 0:
                return low[z + 2, s]
            if z < 2:
                return own[z, s]
            if z < 4:
                return high[z - 2, s]
            return high2[0, s]

        for z in range(-3, 5):
            value = plane(z)
            total = beside_plane(value) - 6.0 * value
            if z > -3:
                total = total + plane(z - 1)
            if z < 4:
                total = total + plane(z + 1)
            g0[z + 3] = total
        for z in range(-2, 4):
            value = g0[z + 3]
            g1[z + 2] = (beside_plane(value) + (g0[z + 2] + g0[z + 4])) * sixth
        moments = [None] * 12
        across = None

        def put(k, value):
            value = folded(value)
            moments[k] = value if moments[k] is None else moments[k] + value

        for z in range(-1, 3):
            value = g1[z + 2]
            g2[z + 1] = (beside_plane(value) + (g1[z + 1] + g1[z + 3])) * sixth
        third = 1.0 / 3.0
        for z in range(2):
            a, b, c = g0[z + 3], g1[z + 2], g2[z + 1]
            basis[0, z, s] = a
            basis[1, z, s] = b
            basis[2, z, s] = c
            put(0, a * a)
            put(1, a * b)
            put(2, b * b)
            put(3, b * c)
            put(4, c * c)
            put(5, c * (beside_plane(c) * sixth + third * g2[z + 2]))
            weight = 1.0 / (1.0 + 0.1 * jnp.abs(state[z, s]))
            a, b, c = a * weight, b * weight, c * weight
            put(6, a * a)
            put(7, a * b)
            put(8, a * c)
            put(9, b * b)
            put(10, b * c)
            put(11, c * c)
        reach = third / 36.0
        put(5, reach * (plane(3) * g2[0] + (1.0 / 36.0) * (far[0, s] * plane(-1))))
        for k in range(12):
            rows[pl.ds(k * STRIDE + s, 1), :] = jnp.sum(moments[k], axis=0, keepdims=True)
        return carry

    lax.fori_loop(0, half, species, 0)
    summed = jnp.sum(jnp.transpose(rows[...]), axis=0, keepdims=True)
    sums[...] = jnp.broadcast_to(summed, sums.shape)


def steps_kernel(parts, coef, own, basis, kept, sent, rms, *, cells):
    devices = parts.shape[0]
    half = own.shape[1]
    mine = lax.axis_index("gz") % 2
    total = parts[0:8, :]
    for d in range(8, devices, 8):
        total = total + parts[d : d + 8, :]
    total = total + pltpu.roll(total, 2, 0)
    total = total + pltpu.roll(total, 4, 0)
    m = [total if k == 0 else pltpu.roll(total, 128 - k * STRIDE, 1) for k in range(12)]
    six_c = 6.0 * coef[...]
    c = coef[...]
    diag = 1.0 + six_c
    smallest = 1.0 / (1.0 + 2.0 * six_c)

    def inner(p, q, shift):
        result = None
        for i, pi in enumerate(p):
            for j, qj in enumerate(q):
                term = pi * qj * m[i + j + shift]
                result = term if result is None else result + term
        return result

    def times(p):
        zero = jnp.zeros_like(c)
        return [diag * a - six_c * b for a, b in zip(list(p) + [zero], [zero] + list(p))]

    residual = [jnp.ones_like(c)]
    direction = list(residual)
    norm_now = m[0]
    answer = [jnp.zeros_like(c)] * 3
    for iteration in range(3):
        energy = diag * inner(direction, direction, 0) - six_c * inner(direction, direction, 1)
        step = jnp.minimum(jnp.maximum(norm_now / energy, smallest), 1.0)
        answer = [a + step * d for a, d in zip(answer, direction + [jnp.zeros_like(c)] * 3)]
        if iteration + 1 < 3:
            image = times(direction)
            residual = [a - step * b for a, b in zip(residual + [jnp.zeros_like(c)], image)]
            norm_next = jnp.maximum(inner(residual, residual, 0), 0.0)
            beta = norm_next / norm_now
            direction = [a + beta * b for a, b in zip(residual, direction + [jnp.zeros_like(c)])]
            norm_now = norm_next
    answer = [c * a for a in answer]
    y0, y1, y2 = answer
    error = (
        y0 * y0 * m[6]
        + y1 * y1 * m[9]
        + y2 * y2 * m[11]
        + 2.0 * (y0 * y1 * m[7] + y0 * y2 * m[8] + y1 * y2 * m[10])
    )
    row = lax.broadcasted_iota(jnp.int32, c.shape, 0)
    col = lax.broadcasted_iota(jnp.int32, c.shape, 1)
    error = jnp.sum(jnp.where((row < 2) & (col < half), error, 0.0), keepdims=True)
    rms[...] = jnp.sqrt(jnp.maximum(error, 0.0) * (1.0 / cells))
    for s in range(half):
        chosen = (row == mine) & (col == s)
        w = [jnp.sum(jnp.where(chosen, y, 0.0)) for y in answer]
        for z, out in ((mine, kept), (1 - mine, sent)):
            out[s] = own[z, s] + (
                w[0] * basis[0, z, s] + (w[1] * basis[1, z, s] + w[2] * basis[2, z, s])
            )


def shards(state, explicit_rhs, implicit_rhs, implicit_coef):
    count = lax.axis_size("gz")
    species, planes, ny, nx = state.shape
    half = species // 2
    assert planes == 1 and species % 2 == 0 and count % 8 == 0 and half <= STRIDE
    vmem = pl.BlockSpec(memory_space=pltpu.VMEM)

    def move(value, shift):
        return lax.ppermute(value, "gz", [(i, (i + shift) % count) for i in range(count)])

    def swap(value):
        return lax.ppermute(value, "gz", [(i, i ^ 1) for i in range(count)])

    section_in = (
        state + explicit_weights[0] * explicit_rhs[0] + explicit_weights[1] * explicit_rhs[1]
    )
    section_in = (
        section_in + implicit_weights[0] * implicit_rhs[0] + implicit_weights[1] * implicit_rhs[1]
    )
    section_in = section_in[:, 0]
    odd = lax.axis_index("gz") % 2

    def paired(field):
        keep = jnp.where(odd == 0, field[:half], field[half:])
        give = jnp.where(odd == 0, field[half:], field[:half])
        take = swap(give)
        return jnp.stack([jnp.where(odd == 0, keep, take), jnp.where(odd == 0, take, keep)])

    own = paired(section_in)
    low = move(own, 2)
    high = move(own, -2)
    low2 = move(own[1:], 4)
    high2 = move(own[:1], -4)
    far = move(own[:1], 8)
    weight_state = paired(state[:, 0])
    basis, sums = pl.pallas_call(
        moments_kernel,
        in_specs=[vmem] * 7,
        out_specs=[vmem] * 2,
        out_shape=[
            jax.ShapeDtypeStruct((3,) + own.shape, jnp.float32),
            jax.ShapeDtypeStruct((count, 128), jnp.float32),
        ],
        scratch_shapes=[
            pltpu.VMEM((8, ny, nx), jnp.float32),
            pltpu.VMEM((6, ny, nx), jnp.float32),
            pltpu.VMEM((4, ny, nx), jnp.float32),
            pltpu.VMEM((128, 128), jnp.float32),
        ],
        name="moments",
    )(own, low, high, low2, high2, far, weight_state)
    parts = lax.all_to_all(sums, "gz", 0, 0)
    coef = jnp.tile(jnp.pad(implicit_coef.reshape(2, half), ((0, 0), (0, 128 - half)), constant_values=1.0), (4, 1))
    cells = species * count * ny * nx
    kept, sent, rms = pl.pallas_call(
        lambda *refs: steps_kernel(*refs, cells=cells),
        in_specs=[vmem] * 4,
        out_specs=[vmem] * 3,
        out_shape=[
            jax.ShapeDtypeStruct((half, ny, nx), jnp.float32),
            jax.ShapeDtypeStruct((half, ny, nx), jnp.float32),
            jax.ShapeDtypeStruct((1, 1), jnp.float32),
        ],
        name="steps",
    )(parts, coef, own, basis)
    taken = swap(sent)
    solution = jnp.concatenate(
        [jnp.where(odd == 0, kept, taken), jnp.where(odd == 0, taken, kept)]
    )
    return (solution[:, None], rms[0, 0])


def solution(mesh):
    placed = (
        P(None, "gz", None, None),
        P(None, None, "gz", None, None),
        P(None, None, "gz", None, None),
        P(),
    )
    return jax.shard_map(
        shards,
        mesh=mesh,
        in_specs=placed,
        out_specs=(P(None, "gz", None, None), P()),
        check_vma=False,
    )
```

time: 232 us -> 68.2 us (0.29)
  blocking collectives: 173 us -> 0 us
  Pallas kernels: 0 us -> 9.29 us
  waiting for transfers between devices: 27.7 us -> 34.6 us
  starting transfers between devices: 22.8 us -> 16.2 us
  local copies, waits for them, and re-layouts: 0.01 us -> 2.34 us
    psum x4 -> x0, blocking collectives: 173 us -> none  [the longest x3 132 us: paired_totals(): lax.psum((species_sum(residual, residual), species_sum(residual, image)),...]
    ppermute x8, starting transfers between devices: 22.8 us -> 12.3 us  [the longest x5 11.7 us: move(): lax.ppermute(value, 'gz', [(i, (i + shift) % count) for i in range(count)])]
    pallas_call x0 -> x2, Pallas kernels: none -> 9.29 us  [the longest x1 6.56 us: shards(): pl.pallas_call(moments_kernel, in_specs=[vmem] * 7, out_specs=[vmem] * 2,...]
    all_to_all x0 -> x1, waiting for transfers between devices: none -> 7.07 us  [shards(): parts = lax.all_to_all(sums, 'gz', 0, 0)]
    all_to_all x0 -> x1, starting transfers between devices: none -> 3.84 us  [shards(): parts = lax.all_to_all(sums, 'gz', 0, 0)]
    reduce_sum x4 -> x0, other arithmetic: 3.39 us -> none  [the longest x1 1.71 us: shards(): summed = lax.psum(jnp.sum(scaled * scaled), 'gz')]
  transfers between devices with their start and end apart: 8 -> 9, of which waited for: 4 -> 6; matrix products, arithmetic and copies ran while one was open for 0% -> 2% of each run, Pallas kernels for 0% -> 0%
where the time goes in v1:
time: 68.2 us; the launch traced here: 68 us
  waiting for transfers between devices  34.6 us (51%)
  starting transfers between devices  16.2 us (24%)
  Pallas kernels  9.29 us (14%)
  other arithmetic  4.78 us (7%)
  local copies, waits for them, and re-layouts  2.34 us (3%)
  between operations  0.76 us (1%)
    ppermute x5, waiting for transfers between devices, move(): lax.ppermute(value, 'gz', [(i, (i + shift) % count) for i in range(count)])  24.8 us
    ppermute x5, starting transfers between devices, move(): lax.ppermute(value, 'gz', [(i, (i + shift) % count) for i in range(count)])  11.7 us
    all_to_all x1, waiting for transfers between devices, shards(): parts = lax.all_to_all(sums, 'gz', 0, 0)  7.07 us
    pallas_call x1, Pallas kernels, shards(): pl.pallas_call(moments_kernel, in_specs=[vmem] * 7, out_specs=[vmem] * 2,...  6.56 us
    all_to_all x1, starting transfers between devices, shards(): parts = lax.all_to_all(sums, 'gz', 0, 0)  3.84 us
    ppermute x3, waiting for transfers between devices, swap(): return lax.ppermute(value, 'gz', [(i, i ^ 1) for i in range(count)])  2.78 us
    pallas_call x1, Pallas kernels, shards(): pl.pallas_call(lambda *refs: steps_kernel(*refs, cells=cells), in_specs=[...  2.73 us
    add x1, other arithmetic, shards(): section_in + implicit_weights[0] * implicit_rhs[0]  1.92 us
  transfers between devices with their start and end apart: 9, of which 6 were waited for; matrix products, arithmetic and copies ran while one was open for 2% of the time, Pallas kernels for 0%

profile of v1, /device:TPU:0, one launch (start us, length us, event | category | flops | bytes accessed | tf_op | source)
XLA Modules:
  0.0 68.0 jit_solution(7805434496156494080)
XLA Ops:
  0.6 0.0 copy-start
  0.7 1.9 %fusion.1 = f32[8,1,64,256]{3,2,0,1:T(8,128)S(1)} fusion(f32[2,8,1,64,256]{4,3,1,2,0:T(8,128)} %bitcast.64, f32[2,8,1,64,256]{4,3,1,2,0:T(8,128)} %bitcast.65, f32[8,1,64,256]{3,2,1,0:T(8,128)} %param.4), kind=kLoop, calls=%fused_computation.2 | loop fusion | flops 1048576 | bytes 3145728 | tf_op jit(solution)/shard_map/add | solution.py:184
  2.6 0.6 collective-permute-start
  3.2 0.0 copy-done
  3.2 0.1 collective-permute-start.6
  3.3 1.0 %collective-permute-done = f32[4,64,256]{2,1,0:T(8,128)S(1)} collective-permute-done((f32[4,64,256]{2,1,0:T(8,128)S(1)}, f32[4,64,256]{2,1,0:T(8,128)S(1)}, u32[]{:S(2)}, u32[]{:S(2)}) %collective-permute-start) | collective-permute-done | bytes 262176 | tf_op jit(solution)/shard_map/ppermute | solution.py:178
  4.3 0.1 fusion.10
  4.4 0.0 copy-start.1
  4.5 2.9 %collective-permute-start.1 = (f32[2,4,64,256]{3,2,1,0:T(8,128)S(1)}, f32[2,4,64,256]{3,2,1,0:T(8,128)S(1)}, u32[]{:S(2)}, u32[]{:S(2)}) collective-permute-start(f32[2,4,64,256]{3,2,1,0:T(8,128)S(1)} %pad_maximum_fusion.own.refs_2_), channel_id=1, source_target_pairs={{0,2},{1,3},{2,4},{3,5},{4,6},{5,7},{6,8},{7,9},{8,10},{9,11},{10,... | collective-permute-start | bytes 1572872 | tf_op jit(solution)/shard_map/ppermute | solution.py:175
  7.4 4.1 %collective-permute-start.2 = (f32[2,4,64,256]{3,2,1,0:T(8,128)S(1)}, f32[2,4,64,256]{3,2,1,0:T(8,128)S(1)}, u32[]{:S(2)}, u32[]{:S(2)}) collective-permute-start(f32[2,4,64,256]{3,2,1,0:T(8,128)S(1)} %pad_maximum_fusion.own.refs_2_), channel_id=1, source_target_pairs={{0,30},{1,31},{2,0},{3,1},{4,2},{5,3},{6,4},{7,5},{8,6},{9,7},{10,... | collective-permute-start | bytes 1572872 | tf_op jit(solution)/shard_map/ppermute | solution.py:175
  11.4 0.0 collective-permute-start.3
  11.4 4.7 %collective-permute-start.4 = (f32[1,4,64,256]{3,2,1,0:T(8,128)S(1)}, f32[1,4,64,256]{3,2,1,0:T(8,128)S(1)}, u32[]{:S(2)}, u32[]{:S(2)}) collective-permute-start(f32[1,4,64,256]{3,2,1,0:T(8,128)S(1)} %get-tuple-element.18), channel_id=1, source_target_pairs={{0,28},{1,29},{2,30},{3,31},{4,0},{5,1},{6,2},{7,3},{8,4},{9,5},{1... | collective-permute-start | bytes 786440 | tf_op jit(solution)/shard_map/ppermute | solution.py:175
  16.1 0.0 collective-permute-done.6
  16.1 0.0 collective-permute-start.5
  16.1 0.1 fusion.8
  16.2 0.8 %pad_maximum_fusion.1.state = f32[2,4,64,256]{3,2,1,0:T(8,128)} fusion(f32[1,4,64,256]{3,2,1,0:T(8,128)S(1)} %get-tuple-element.17, f32[1,4,64,256]{3,2,1,0:T(8,128)S(1)} %get-tuple-element.16), kind=kLoop, calls=%fused_computation.13 | loop fusion | flops 131072 | bytes 1048576 | tf_op jit(solution)/shard_map/stack | solution.py:193
  17.0 0.0 copy-start.8
  17.0 11.9 %collective-permute-done.3.low2 = f32[1,4,64,256]{3,2,1,0:T(8,128)S(1)} collective-permute-done((f32[1,4,64,256]{3,2,1,0:T(8,128)S(1)}, f32[1,4,64,256]{3,2,1,0:T(8,128)S(1)}, u32[]{:S(2)}, u32[]{:S(2)}) %collective-permute-start.3) | collective-permute-done | bytes 262176 | tf_op jit(solution)/shard_map/ppermute | solution.py:175
  29.0 0.0 copy-start.4
  29.0 5.9 %collective-permute-done.4.high2 = f32[1,4,64,256]{3,2,1,0:T(8,128)S(1)} collective-permute-done((f32[1,4,64,256]{3,2,1,0:T(8,128)S(1)}, f32[1,4,64,256]{3,2,1,0:T(8,128)S(1)}, u32[]{:S(2)}, u32[]{:S(2)}) %collective-permute-start.4) | collective-permute-done | bytes 262176 | tf_op jit(solution)/shard_map/ppermute | solution.py:175
  34.9 0.0 copy-start.5
  34.9 6.9 %collective-permute-done.5.far = f32[1,4,64,256]{3,2,1,0:T(8,128)S(1)} collective-permute-done((f32[1,4,64,256]{3,2,1,0:T(8,128)S(1)}, f32[1,4,64,256]{3,2,1,0:T(8,128)S(1)}, u32[]{:S(2)}, u32[]{:S(2)}) %collective-permute-start.5) | collective-permute-done | bytes 262176 | tf_op jit(solution)/shard_map/ppermute | solution.py:175
  41.8 0.0 copy-start.6
  41.8 0.0 collective-permute-done.1.low
  41.8 0.0 copy-start.2
  41.8 0.0 collective-permute-done.2.high
  41.8 0.0 copy-done.1
  41.8 0.0 copy-done.4
  41.8 0.0 copy-done.5
  41.8 0.6 copy-done.6
  42.5 0.2 copy-done.2
  42.7 0.0 copy-start.3
  42.7 0.8 %copy-done.3 = f32[2,4,64,256]{3,2,1,0:T(8,128)} copy-done((f32[2,4,64,256]{3,2,1,0:T(8,128)}, f32[2,4,64,256]{3,2,1,0:T(8,128)S(1)}, u32[]{:S(2)}) %copy-start.3) | copy-done | bytes 524312
  43.5 6.6 %moments.1 = (f32[3,2,4,64,256]{4,3,2,1,0:T(8,128)}, f32[32,128]{1,0:T(8,128)}) custom-call(f32[2,4,64,256]{3,2,1,0:T(8,128)} %copy-done.1, f32[2,4,64,256]{3,2,1,0:T(8,128)} %copy-done.2, f32[2,4,64,256]{3,2,1,0:T(8,128)} %copy-done.3, f32[1,4,64,256]{3,2,1,0:T(8,128)} %copy-done.4, f32[1,4,64,256]{3,2,1,0:T(8,128)} %copy-done.5, ...), custom_call_target="tpu_custom_call" | custom-call | tf_op jit(solution)/shard_map/moments/pallas_call | solution.py:202
  50.0 3.8 %all-to-all-start = ((f32[32,1,128]{2,1,0:T(1,128)}), f32[32,1,128]{2,1,0:T(1,128)S(1)}, u32[]{:S(2)}, u32[]{:S(2)}) async-start(f32[32,1,128]{2,1,0:T(1,128)} %bitcast.68), calls=%async_computation | async-start | bytes 32768 | tf_op jit(solution)/shard_map/all_to_all | solution.py:218
  53.9 0.0 copy-done.8
  53.9 0.1 reshape.81
  54.0 7.1 %all-to-all-done = f32[32,1,128]{2,1,0:T(1,128)S(1)} async-done(((f32[32,1,128]{2,1,0:T(1,128)}), f32[32,1,128]{2,1,0:T(1,128)S(1)}, u32[]{:S(2)}, u32[]{:S(2)}) %all-to-all-start) | async-done | bytes 16416 | tf_op jit(solution)/shard_map/all_to_all | solution.py:218
  61.1 0.0 copy-start.7
  61.1 0.6 tile.4
  61.7 0.0 copy-done.7
  61.7 2.7 %steps.1 = (f32[4,64,256]{2,1,0:T(8,128)}, f32[4,64,256]{2,1,0:T(8,128)}, f32[1,1]{1,0:T(1,128)}) custom-call(f32[32,128]{1,0:T(8,128)} %bitcast.66, f32[8,128]{1,0:T(8,128)} %bitcast.67, f32[2,4,64,256]{3,2,1,0:T(8,128)} %copy-done.1, f32[3,2,4,64,256]{4,3,2,1,0:T(8,128)} %get-tuple-element.8.refs_3_), custom_call_target="tpu_custom_call" | custom-call | tf_op jit(solution)/shard_map/steps/pallas_call | solution.py:221
  64.4 0.0 collective-permute-start.7
  64.4 1.7 %collective-permute-done.7 = f32[4,64,256]{2,1,0:T(8,128)S(1)} collective-permute-done((f32[4,64,256]{2,1,0:T(8,128)}, f32[4,64,256]{2,1,0:T(8,128)S(1)}, u32[]{:S(2)}, u32[]{:S(2)}) %collective-permute-start.7) | collective-permute-done | bytes 262176 | tf_op jit(solution)/shard_map/ppermute | solution.py:178
  66.1 1.0 %broadcast_select_fusion.1 = (f32[4,64,256]{2,1,0:T(8,128)S(1)}, f32[4,64,256]{2,1,0:T(8,128)S(1)}) fusion(f32[4,64,256]{2,1,0:T(8,128)} %get-tuple-element.9, f32[4,64,256]{2,1,0:T(8,128)S(1)} %collective-permute-done.7, pred[]{:T(512)S(6)} %eq.4), kind=kLoop, calls=%fused_computation.28 | loop fusion | flops 131072 | bytes 1048577 | tf_op jit(solution)/shard_map/jit(_where)/select_n | solution.py:234
  67.1 0.8 %maximum_bitcast_fusion = f32[8,1,64,256]{3,2,1,0:T(8,128)} fusion(f32[4,64,256]{2,1,0:T(8,128)S(1)} %get-tuple-element.21, f32[4,64,256]{2,1,0:T(8,128)S(1)} %get-tuple-element.20), kind=kLoop, calls=%fused_computation.14 | loop fusion | flops 131072 | bytes 1048576
  (4 shorter events, 0.1 us)
Async XLA Ops:
  0.6 2.5 %copy-start = (f32[8,1,64,256]{3,2,1,0:T(8,128)S(1)}, f32[8,1,64,256]{3,2,1,0:T(8,128)}, u32[]{:S(2)}) copy-start(f32[8,1,64,256]{3,2,1,0:T(8,128)} %param.4) | copy-start | bytes 1572868
  2.6 1.7 %collective-permute-start = (f32[4,64,256]{2,1,0:T(8,128)S(1)}, f32[4,64,256]{2,1,0:T(8,128)S(1)}, u32[]{:S(2)}, u32[]{:S(2)}) collective-permute-start(f32[4,64,256]{2,1,0:T(8,128)S(1)} %select_bitcast_fusion.1), channel_id=1, source_target_pairs={{0,1},{1,0},{2,3},{3,2},{4,5},{5,4},{6,7},{7,6},{8,9},{9,8},{10,11... | collective-permute-start | bytes 786440 | tf_op jit(solution)/shard_map/ppermute | solution.py:178
  3.2 12.9 %collective-permute-start.6 = (f32[4,64,256]{2,1,0:T(8,128)S(1)}, f32[4,64,256]{2,1,0:T(8,128)S(1)}, u32[]{:S(2)}, u32[]{:S(2)}) collective-permute-start(f32[4,64,256]{2,1,0:T(8,128)S(1)} %select_bitcast_fusion), channel_id=1, source_target_pairs={{0,1},{1,0},{2,3},{3,2},{4,5},{5,4},{6,7},{7,6},{8,9},{9,8},{10,11... | collective-permute-start | bytes 786440 | tf_op jit(solution)/shard_map/ppermute | solution.py:178
  4.4 37.4 %copy-start.1 = (f32[2,4,64,256]{3,2,1,0:T(8,128)}, f32[2,4,64,256]{3,2,1,0:T(8,128)S(1)}, u32[]{:S(2)}) copy-start(f32[2,4,64,256]{3,2,1,0:T(8,128)S(1)} %pad_maximum_fusion.own.refs_2_) | copy-start | bytes 1572868
  4.5 37.3 %collective-permute-start.1 = (f32[2,4,64,256]{3,2,1,0:T(8,128)S(1)}, f32[2,4,64,256]{3,2,1,0:T(8,128)S(1)}, u32[]{:S(2)}, u32[]{:S(2)}) collective-permute-start(f32[2,4,64,256]{3,2,1,0:T(8,128)S(1)} %pad_maximum_fusion.own.refs_2_), channel_id=1, source_target_pairs={{0,2},{1,3},{2,4},{3,5},{4,6},{5,7},{6,8},{7,9},{8,10},{9,11},{10,... | collective-permute-start | bytes 1572872 | tf_op jit(solution)/shard_map/ppermute | solution.py:175
  7.4 34.5 %collective-permute-start.2 = (f32[2,4,64,256]{3,2,1,0:T(8,128)S(1)}, f32[2,4,64,256]{3,2,1,0:T(8,128)S(1)}, u32[]{:S(2)}, u32[]{:S(2)}) collective-permute-start(f32[2,4,64,256]{3,2,1,0:T(8,128)S(1)} %pad_maximum_fusion.own.refs_2_), channel_id=1, source_target_pairs={{0,30},{1,31},{2,0},{3,1},{4,2},{5,3},{6,4},{7,5},{8,6},{9,7},{10,... | collective-permute-start | bytes 1572872 | tf_op jit(solution)/shard_map/ppermute | solution.py:175
  11.4 17.6 %collective-permute-start.3 = (f32[1,4,64,256]{3,2,1,0:T(8,128)S(1)}, f32[1,4,64,256]{3,2,1,0:T(8,128)S(1)}, u32[]{:S(2)}, u32[]{:S(2)}) collective-permute-start(f32[1,4,64,256]{3,2,1,0:T(8,128)S(1)} %get-tuple-element.19), channel_id=1, source_target_pairs={{0,4},{1,5},{2,6},{3,7},{4,8},{5,9},{6,10},{7,11},{8,12},{9,13},{1... | collective-permute-start | bytes 786440 | tf_op jit(solution)/shard_map/ppermute | solution.py:175
  11.4 23.5 %collective-permute-start.4 = (f32[1,4,64,256]{3,2,1,0:T(8,128)S(1)}, f32[1,4,64,256]{3,2,1,0:T(8,128)S(1)}, u32[]{:S(2)}, u32[]{:S(2)}) collective-permute-start(f32[1,4,64,256]{3,2,1,0:T(8,128)S(1)} %get-tuple-element.18), channel_id=1, source_target_pairs={{0,28},{1,29},{2,30},{3,31},{4,0},{5,1},{6,2},{7,3},{8,4},{9,5},{1... | collective-permute-start | bytes 786440 | tf_op jit(solution)/shard_map/ppermute | solution.py:175
  16.1 25.7 %collective-permute-start.5 = (f32[1,4,64,256]{3,2,1,0:T(8,128)S(1)}, f32[1,4,64,256]{3,2,1,0:T(8,128)S(1)}, u32[]{:S(2)}, u32[]{:S(2)}) collective-permute-start(f32[1,4,64,256]{3,2,1,0:T(8,128)S(1)} %get-tuple-element.18), channel_id=1, source_target_pairs={{0,8},{1,9},{2,10},{3,11},{4,12},{5,13},{6,14},{7,15},{8,16},{9,17... | collective-permute-start | bytes 786440 | tf_op jit(solution)/shard_map/ppermute | solution.py:175
  17.0 36.9 %copy-start.8 = (f32[8]{0:T(128)S(1)}, f32[8]{0:T(128)}, u32[]{:S(2)}) copy-start(f32[8]{0:T(128)} %param.7) | copy-start | bytes 100
  29.0 12.9 %copy-start.4 = (f32[1,4,64,256]{3,2,1,0:T(8,128)}, f32[1,4,64,256]{3,2,1,0:T(8,128)S(1)}, u32[]{:S(2)}) copy-start(f32[1,4,64,256]{3,2,1,0:T(8,128)S(1)} %collective-permute-done.3.low2) | copy-start | bytes 786436
  34.9 6.9 %copy-start.5 = (f32[1,4,64,256]{3,2,1,0:T(8,128)}, f32[1,4,64,256]{3,2,1,0:T(8,128)S(1)}, u32[]{:S(2)}) copy-start(f32[1,4,64,256]{3,2,1,0:T(8,128)S(1)} %collective-permute-done.4.high2) | copy-start | bytes 786436
  41.8 0.7 %copy-start.6 = (f32[1,4,64,256]{3,2,1,0:T(8,128)}, f32[1,4,64,256]{3,2,1,0:T(8,128)S(1)}, u32[]{:S(2)}) copy-start(f32[1,4,64,256]{3,2,1,0:T(8,128)S(1)} %collective-permute-done.5.far) | copy-start | bytes 786436
  41.8 0.9 %copy-start.2 = (f32[2,4,64,256]{3,2,1,0:T(8,128)}, f32[2,4,64,256]{3,2,1,0:T(8,128)S(1)}, u32[]{:S(2)}) copy-start(f32[2,4,64,256]{3,2,1,0:T(8,128)S(1)} %collective-permute-done.1.low) | copy-start | bytes 1572868
  42.7 0.8 %copy-start.3 = (f32[2,4,64,256]{3,2,1,0:T(8,128)}, f32[2,4,64,256]{3,2,1,0:T(8,128)S(1)}, u32[]{:S(2)}) copy-start(f32[2,4,64,256]{3,2,1,0:T(8,128)S(1)} %collective-permute-done.2.high) | copy-start | bytes 1572868
  50.0 11.0 %all-to-all-start = ((f32[32,1,128]{2,1,0:T(1,128)}), f32[32,1,128]{2,1,0:T(1,128)S(1)}, u32[]{:S(2)}, u32[]{:S(2)}) async-start(f32[32,1,128]{2,1,0:T(1,128)} %bitcast.68), calls=%async_computation | async-start | bytes 32768 | tf_op jit(solution)/shard_map/all_to_all | solution.py:218
  61.1 0.6 copy-start.7
  64.4 1.7 %collective-permute-start.7 = (f32[4,64,256]{2,1,0:T(8,128)}, f32[4,64,256]{2,1,0:T(8,128)S(1)}, u32[]{:S(2)}, u32[]{:S(2)}) collective-permute-start(f32[4,64,256]{2,1,0:T(8,128)} %get-tuple-element.10), channel_id=1, source_target_pairs={{0,1},{1,0},{2,3},{3,2},{4,5},{5,4},{6,7},{7,6},{8,9},{9,8},{10,11... | collective-permute-start | bytes 786440 | tf_op jit(solution)/shard_map/ppermute | solution.py:178
